TPU v7x, 256 devices: a whole 4x4x8 slice. The times are simulated.
256 devices in a mesh: dp: 8 (over x, core), expert: 32 (over z, y).
Axes of the slice: x: 4, y: 4, z: 8, core: 2. Of those that a mesh axis runs over, the one named last changes fastest.
Arguments:
- tokens: bfloat16 [5120, 262144], P(None, ('dp', 'expert')), may hold values from -24 to 24, as said below
- router: bfloat16 [5120, 160], P(None, 'expert'), may hold values from -1 to 1, as said below
- device_pick: int32 [3, 262144], P(None, 'dp'), may hold values from 0 to 31, as said below
- expert_pick: int32 [6, 262144], P(None, 'dp'), may hold values from 0 to 159, as said below
Outputs:
- gates: float32 [6, 262144], P(None, 'dp')
- device_max: float32 [32, 262144], P('expert', 'dp')
- balance: float32 [3], replicated
Inputs may be any that keep to these rules, and one draw needn't show every extreme that they name: tokens lie within the range; in each column the values are of order one, except in a few columns. router entries are of order 1 / sqrt(5120). `device_pick`: each column names 3 different devices. `expert_pick`: each column names 6 different experts, two on each device of the column's device_pick, in that order; the device of expert e is e // 5.
All inputs are finite; a program needn't handle non-finite values.
Results may differ from a plain program's by a relative error of at most 0.0003.
Values may be sent and summed in bfloat16 or wider, within the bound.
A program may use at most 64 MiB of HBM per device.

v0:
```python
import functools

import jax
import jax.numpy as jnp
from jax import lax
from jax.experimental import pallas as pl
from jax.experimental.pallas import tpu as pltpu
from jax.sharding import PartitionSpec as P

MESH = pl.DeviceIdType.MESH
TOP = 6
DEV_TOP = 3
SLOT = 8
LOG2E = 1.4426950408889634
GATE_SCALE = 2048.0
NEG = -1e30
VMEM = 67043328


def kernel(
    sizes, tokens, router, device_pick, expert_pick,
    recv_msg, balance,
    tok, raw, own_rows, rows, picks, dpicks, sent_msg, cnt_msg, cnt_recv, bal_msg, bal_recv, prob_acc,
    tok_sem, pick_sem, rs_sem, rr_sem, ys_sem, yr_sem, ps_sem, pr_sem,
    ms_sem, mr_sem, fs_sem, fr_sem, cs_sem, cr_sem, bs_sem, br_sem,
):
    ndp, ndev, per_dev, width, chunks = sizes
    depth = tokens.shape[0]
    share = tokens.shape[1]
    total = share * ndev * ndp
    nrows = ndev * SLOT
    everyone = ndp * ndev
    half = depth // 2
    dp, me = lax.axis_index("dp"), lax.axis_index("expert")
    lin = dp * ndev + me
    core = lax.rem(dp, 2)
    partner = dp + 1 - 2 * core

    def token_copy(c):
        return pltpu.make_async_copy(
            tokens.at[:, pl.ds(pl.multiple_of(c * width, width), width)], tok.at[c], tok_sem.at[c]
        )

    mine = pl.ds(pl.multiple_of(me * share, share), share)
    pick_copy = pltpu.make_async_copy(expert_pick.at[:, mine], picks, pick_sem.at[0])
    dpick_copy = pltpu.make_async_copy(device_pick.at[:, mine], dpicks, pick_sem.at[1])
    raw_copy = pltpu.make_async_copy(router, raw, pick_sem.at[2])
    raw_copy.start()
    pick_copy.start()
    dpick_copy.start()
    for c in range(chunks):
        token_copy(c).start()

    barrier = pltpu.get_barrier_semaphore()

    def other(j):
        t = lax.rem(lin + j, everyone)
        return (t // ndev, lax.rem(t, ndev))

    def greet(j, carry):
        pl.semaphore_signal(barrier, inc=1, device_id=other(j), device_id_type=MESH)
        return carry

    lax.fori_loop(1, everyone, greet, 0)
    raw_copy.wait()
    pad = jnp.zeros((SLOT - per_dev, depth), jnp.float32)
    own_rows[...] = jnp.concatenate([raw[...].astype(jnp.float32), pad], axis=0).astype(jnp.bfloat16)
    pl.semaphore_wait(barrier, everyone - 1)

    pairs = ndev // 2
    my_pair, side = me // 2, lax.rem(me, 2)
    mate = me + 1 - 2 * side

    def ahead(j):
        return lax.rem(my_pair + j, pairs) * 2 + side

    def behind(j, which):
        return lax.rem(my_pair + pairs - j, pairs) * 2 + which

    my_half = pl.ds(pl.multiple_of(core * half, half), half)
    my_rows = pl.ds(pl.multiple_of(me * SLOT, SLOT), SLOT)

    def slot(src):
        return rows.at[pl.ds(pl.multiple_of(src * SLOT, SLOT), SLOT), my_half]

    def router_copy(j):
        return pltpu.make_async_remote_copy(
            src_ref=own_rows.at[:, my_half], dst_ref=slot(me),
            send_sem=rs_sem.at[j], recv_sem=rr_sem.at[j], device_id=(dp, ahead(j)), device_id_type=MESH,
        )

    def mate_copy(j):
        return pltpu.make_async_remote_copy(
            src_ref=own_rows.at[:, my_half] if j == 0 else slot(behind(j, side)), dst_ref=slot(behind(j, side)),
            send_sem=ys_sem.at[j], recv_sem=yr_sem.at[j], device_id=(dp, mate), device_id_type=MESH,
        )

    def partner_copy(j, other_side):
        block = slot(behind(j, 1 - side if other_side else side))
        spot = j + other_side * pairs
        return pltpu.make_async_remote_copy(
            src_ref=block, dst_ref=block, send_sem=ps_sem.at[spot], recv_sem=pr_sem.at[spot],
            device_id=(partner, me), device_id_type=MESH,
        )

    for j in range(1, pairs):
        router_copy(j).start()
    mate_copy(0).start()
    own = pltpu.make_async_copy(own_rows, rows.at[my_rows, :], rs_sem.at[0])
    own.start()

    pick_copy.wait()
    dpick_copy.wait()
    row = lax.broadcasted_iota(jnp.int32, (nrows, 128), 0)
    lane = lax.broadcasted_iota(jnp.int32, (nrows, 128), 1)
    one, nil = jnp.float32(1.0), jnp.float32(0.0)
    ids = (row // SLOT) * per_dev + lax.rem(row, SLOT)
    ids = jnp.where(lax.rem(row, SLOT) < per_dev, ids, -1)
    dev_ids = jnp.where(lax.rem(row, SLOT) == 0, row // SLOT, -1)

    def count(i, carry):
        counts, sends = carry
        cols = pl.ds(pl.multiple_of(i * 128, 128), 128)
        for k in range(TOP):
            counts = counts + jnp.where(picks[k : k + 1, cols] == ids, one, nil)
        for k in range(DEV_TOP):
            sends = sends + jnp.where(dpicks[k : k + 1, cols] == dev_ids, one, nil)
        return counts, sends

    zero = jnp.zeros((nrows, 128), jnp.float32)
    counts, sends = lax.fori_loop(0, share // 128, count, (zero, zero))
    counts = jnp.sum(counts, axis=1, keepdims=True)
    sends = jnp.sum(sends, axis=1, keepdims=True)
    pages = cnt_msg.shape[1] // 2 // 128
    for p in range(pages):
        spot = row == lane + p * 128
        cnt_msg[:, p * 128 : (p + 1) * 128] = jnp.sum(jnp.where(spot, counts, nil), axis=0, keepdims=True)
        cnt_msg[:, (pages + p) * 128 : (pages + p + 1) * 128] = jnp.sum(
            jnp.where(spot, sends, nil), axis=0, keepdims=True
        )
    cnt_recv[lin] = cnt_msg[...]

    def count_copy(j):
        return pltpu.make_async_remote_copy(
            src_ref=cnt_msg, dst_ref=cnt_recv.at[lin], send_sem=cs_sem, recv_sem=cr_sem,
            device_id=other(j), device_id_type=MESH,
        )

    def start_count(j, carry):
        count_copy(j).start()
        return carry

    lax.fori_loop(1, everyone, start_count, 0)

    own.wait()
    for j in range(1, pairs):
        router_copy(j).wait_recv()
        mate_copy(j).start()
        partner_copy(j, 0).start()
    for j in range(pairs):
        mate_copy(j).wait_recv()
        partner_copy(j, 1).start()
    for j in range(1, pairs):
        partner_copy(j, 0).wait_recv()
    for j in range(pairs):
        partner_copy(j, 1).wait_recv()

    prob_acc[...] = zero
    wide_row = lax.broadcasted_iota(jnp.int32, (nrows, width), 0)
    wide_ids = (wide_row // SLOT) * per_dev + lax.rem(wide_row, SLOT)
    real = lax.rem(wide_row, SLOT) < per_dev
    wide_ids = jnp.where(real, wide_ids, -1)
    msg_row = lax.broadcasted_iota(jnp.int32, (4, width), 0)

    def message_copy(j, c):
        return pltpu.make_async_remote_copy(
            src_ref=sent_msg.at[lax.rem(my_pair + j, pairs), c], dst_ref=recv_msg.at[me, c],
            send_sem=ms_sem.at[j], recv_sem=mr_sem.at[j, c], device_id=(dp, ahead(j)), device_id_type=MESH,
        )

    def forward_copy(j, c):
        src = behind(j, side)
        return pltpu.make_async_remote_copy(
            src_ref=sent_msg.at[my_pair, c] if j == 0 else recv_msg.at[src, c], dst_ref=recv_msg.at[src, c],
            send_sem=fs_sem.at[j], recv_sem=fr_sem.at[j], device_id=(dp, mate), device_id_type=MESH,
        )

    def forward(c):
        for j in range(1, pairs):
            message_copy(j, c).wait_recv()
            forward_copy(j, c).start()

    def step(c, carry):
        token_copy(c).wait()
        scores = jnp.dot(rows[...], tok[c], preferred_element_type=jnp.float32)
        scores = jnp.where(real, scores, NEG)
        peak = jnp.max(scores, axis=0, keepdims=True)
        shifted = scores - peak
        raised = jnp.exp(shifted)
        norm = jnp.sum(raised, axis=0, keepdims=True)
        probs = raised * (1.0 / norm)
        acc = prob_acc[...]
        for i in range(width // 128):
            acc = acc + probs[:, i * 128 : (i + 1) * 128]
        prob_acc[...] = acc
        log_norm = jnp.log(norm)
        cols = pl.ds(pl.multiple_of(c * width, width), width)
        codes = []
        for k in range(TOP):
            hit = picks[k : k + 1, cols] == wide_ids
            picked = jnp.sum(jnp.where(hit, shifted, nil), axis=0, keepdims=True)
            code = (log_norm - picked) * (LOG2E * GATE_SCALE) + 0.5
            codes.append(jnp.clip(code, 0.0, 65535.0).astype(jnp.int32))
        words = [codes[k] + jnp.left_shift(codes[k + TOP // 2], 16) for k in range(TOP // 2)]
        base = jnp.where(msg_row == 0, words[0], jnp.where(msg_row == 1, words[1], words[2]))
        tops = []
        for d in range(ndev):
            best = jnp.max(shifted[d * SLOT : (d + 1) * SLOT, :], axis=0, keepdims=True)
            code = (log_norm - best) * (LOG2E * GATE_SCALE) + 0.5
            tops.append(jnp.clip(code, 0.0, 65535.0).astype(jnp.int32))
        for p in range(pairs):
            top = tops[2 * p] + jnp.left_shift(tops[2 * p + 1], 16)
            sent_msg[p, c] = jnp.where(msg_row == 3, top, base)
        recv_msg[me, c] = sent_msg[my_pair, c]
        for j in range(1, pairs):
            message_copy(j, c).start()
        forward_copy(0, c).start()

        @pl.when(c >= lag)
        def _():
            forward(c - lag)

        return carry

    lag = min(3, chunks)
    lax.fori_loop(0, chunks, step, 0)

    pltpu.make_async_copy(cnt_recv.at[pl.ds(0, everyone - 1)], cnt_recv.at[pl.ds(0, everyone - 1)], cr_sem).wait()
    all_counts = jnp.sum(cnt_recv[...], axis=0)
    freq = jnp.zeros((nrows, 1), jnp.float32)
    dev_freq = jnp.zeros((nrows, 1), jnp.float32)
    sent = jnp.zeros((nrows, 1), jnp.float32)
    for p in range(pages):
        here = all_counts[:, p * 128 : (p + 1) * 128]
        there = all_counts[:, (pages + p) * 128 : (pages + p + 1) * 128]
        where = lane + p * 128
        same = (where // SLOT) == (row // SLOT)
        freq = freq + jnp.sum(jnp.where(where == row, here, nil), axis=1, keepdims=True)
        dev_freq = dev_freq + jnp.sum(jnp.where(same, here, nil), axis=1, keepdims=True)
        sent = sent + jnp.sum(jnp.where(same, there, nil), axis=1, keepdims=True)
    experts = ndev * per_dev
    freq = freq * (experts / (TOP * total))
    dev_freq = dev_freq * (experts / (TOP * total) / per_dev)
    sent = sent * (ndev / (DEV_TOP * total))
    prob = prob_acc[...] * (1.0 / total)
    one_lane = lax.broadcasted_iota(jnp.int32, (1, 128), 1)
    result = jnp.zeros((1, 128), jnp.float32)
    for i, factor in enumerate((freq, dev_freq, sent)):
        part = jnp.sum(jnp.sum(prob * factor, axis=0, keepdims=True), axis=1, keepdims=True)
        result = jnp.where(one_lane == i, part, result)
    bal_msg[...] = result
    bal_recv[lin] = result

    def bal_copy(j):
        return pltpu.make_async_remote_copy(
            src_ref=bal_msg, dst_ref=bal_recv.at[lin], send_sem=bs_sem, recv_sem=br_sem,
            device_id=other(j), device_id_type=MESH,
        )

    def start_bal(j, carry):
        bal_copy(j).start()
        return carry

    lax.fori_loop(1, everyone, start_bal, 0)

    for c in range(chunks - lag, chunks):
        forward(c)
    for j in range(pairs):
        src = behind(j, 1 - side)
        pltpu.make_async_copy(recv_msg.at[src], recv_msg.at[src], fr_sem.at[j]).wait()

    pltpu.make_async_copy(bal_recv.at[pl.ds(0, everyone - 1)], bal_recv.at[pl.ds(0, everyone - 1)], br_sem).wait()
    balance[...] = jnp.sum(bal_recv[...], axis=0)

    for j in range(pairs):
        if j:
            router_copy(j).wait_send()
            partner_copy(j, 0).wait_send()
            pltpu.make_async_copy(sent_msg.at[0], sent_msg.at[0], ms_sem.at[j]).wait()
        mate_copy(j).wait_send()
        partner_copy(j, 1).wait_send()
        pltpu.make_async_copy(sent_msg.at[0], sent_msg.at[0], fs_sem.at[j]).wait()
    pltpu.make_async_copy(cnt_recv.at[pl.ds(0, everyone - 1)], cnt_recv.at[pl.ds(0, everyone - 1)], cs_sem).wait()
    pltpu.make_async_copy(bal_recv.at[pl.ds(0, everyone - 1)], bal_recv.at[pl.ds(0, everyone - 1)], bs_sem).wait()


def decode(sizes, recv_msg, sums, gates, device_max, balance, gate_buf, top_buf, sem):
    ndev, share, width, chunks = sizes
    side = lax.rem(lax.axis_index("expert"), 2)
    copies = []
    for src in range(ndev):
        block = pl.ds(src * share, share)

        def body(c, carry):
            words = recv_msg[src, c]
            low = jnp.exp2((words & 65535).astype(jnp.float32) * (-1.0 / GATE_SCALE))
            high = jnp.exp2(lax.shift_right_logical(words, 16).astype(jnp.float32) * (-1.0 / GATE_SCALE))
            cols = pl.ds(pl.multiple_of(src * share + c * width, width), width)
            gate_buf[0:3, cols] = low[0:3]
            gate_buf[3:6, cols] = high[0:3]
            top_buf[:, cols] = jnp.where(side == 0, low[3:4], high[3:4])
            return carry

        lax.fori_loop(0, chunks, body, 0)
        copies.append(pltpu.make_async_copy(gate_buf.at[:, block], gates.at[:, block], sem.at[0, src]))
        copies.append(pltpu.make_async_copy(top_buf.at[:, block], device_max.at[:, block], sem.at[1, src]))
        copies[-2].start()
        copies[-1].start()
    lane = lax.broadcasted_iota(jnp.int32, (1, 128), 1)
    for i in range(3):
        balance[i] = jnp.sum(jnp.where(lane == i, sums[...], jnp.float32(0.0)))
    for copy in copies:
        copy.wait()


def local(tokens, router, device_pick, expert_pick):
    depth, share = tokens.shape
    ndev, ndp = lax.axis_size("expert"), lax.axis_size("dp")
    per_dev = router.shape[1]
    width = min(512, share)
    chunks = share // width
    nrows = ndev * SLOT
    padded = (nrows + 127) // 128 * 128
    everyone = ndp * ndev
    pairs = ndev // 2
    dma = pltpu.SemaphoreType.DMA
    messages, sums = pl.pallas_call(
        functools.partial(kernel, (ndp, ndev, per_dev, width, chunks)),
        out_shape=(
            jax.ShapeDtypeStruct((ndev, chunks, 4, width), jnp.int32),
            jax.ShapeDtypeStruct((1, 128), jnp.float32),
        ),
        in_specs=[pl.BlockSpec(memory_space=pltpu.HBM)] * 4,
        out_specs=(pl.BlockSpec(memory_space=pltpu.VMEM), pl.BlockSpec(memory_space=pltpu.VMEM)),
        scratch_shapes=[
            pltpu.VMEM((chunks, depth, width), jnp.bfloat16),
            pltpu.VMEM((per_dev, depth), jnp.bfloat16),
            pltpu.VMEM((SLOT, depth), jnp.bfloat16),
            pltpu.VMEM((nrows, depth), jnp.bfloat16),
            pltpu.VMEM((TOP, share), jnp.int32),
            pltpu.VMEM((DEV_TOP, share), jnp.int32),
            pltpu.VMEM((pairs, chunks, 4, width), jnp.int32),
            pltpu.VMEM((1, 2 * padded), jnp.float32),
            pltpu.VMEM((everyone, 1, 2 * padded), jnp.float32),
            pltpu.VMEM((1, 128), jnp.float32),
            pltpu.VMEM((everyone, 1, 128), jnp.float32),
            pltpu.VMEM((nrows, 128), jnp.float32),
            dma((chunks,)),
            dma((3,)),
            dma((pairs,)),
            dma((pairs,)),
            dma((pairs,)),
            dma((pairs,)),
            dma((2 * pairs,)),
            dma((2 * pairs,)),
            dma((pairs,)),
            dma((pairs, chunks)),
            dma((pairs,)),
            dma((pairs,)),
            dma,
            dma,
            dma,
            dma,
        ],
        compiler_params=pltpu.CompilerParams(
            collective_id=0, has_side_effects=True, vmem_limit_bytes=VMEM - share * ndev * 16 - 10747904
        ),
        name="route",
    )(tokens, router.T, device_pick, expert_pick)
    gates, device_max, balance = pl.pallas_call(
        functools.partial(decode, (ndev, share, width, chunks)),
        out_shape=(
            jax.ShapeDtypeStruct((TOP, share * ndev), jnp.float32),
            jax.ShapeDtypeStruct((1, share * ndev), jnp.float32),
            jax.ShapeDtypeStruct((3,), jnp.float32),
        ),
        in_specs=[pl.BlockSpec(memory_space=pltpu.VMEM)] * 2,
        out_specs=(
            pl.BlockSpec(memory_space=pl.ANY),
            pl.BlockSpec(memory_space=pl.ANY),
            pl.BlockSpec(memory_space=pltpu.SMEM),
        ),
        scratch_shapes=[
            pltpu.VMEM((TOP, share * ndev), jnp.float32),
            pltpu.VMEM((1, share * ndev), jnp.float32),
            dma((2, ndev)),
        ],
        compiler_params=pltpu.CompilerParams(vmem_limit_bytes=8 * 1024 * 1024),
        name="decode",
    )(messages, sums)
    return gates, device_max, balance


def solution(mesh):
    placed = (P(None, ("dp", "expert")), P(None, "expert"), P(None, "dp"), P(None, "dp"))
    return jax.shard_map(
        local,
        mesh=mesh,
        in_specs=placed,
        out_specs=(P(None, "dp"), P("expert", "dp"), P()),
        check_vma=False,
    )
```

profile of v0, /device:TPU:1, one launch (start us, length us, event | category | flops | bytes accessed | tf_op | source)
XLA Modules:
  0.0 73.8 jit_solution(17109224964070542764)
XLA Ops:
  0.6 0.0 copy-start
  0.6 0.9 %copy-done = bf16[5120,5]{0,1:T(8,128)(2,1)S(1)} copy-done((bf16[5120,5]{0,1:T(8,128)(2,1)S(1)}, bf16[5120,5]{0,1:T(8,128)(2,1)}, u32[]{:S(2)}) %copy-start) | copy-done | bytes 51224
  1.5 69.5 %route.1 = (s32[32,2,4,512]{3,2,1,0:T(4,128)S(1)}, f32[1,128]{1,0:T(1,128)S(1)}) custom-call(bf16[5120,1024]{1,0:T(8,128)(2,1)} %tokens.1, bf16[5,5120]{1,0:T(8,128)(2,1)S(1)} %bitcast.1, s32[3,32768]{1,0:T(4,128)} %device_pick.1, s32[6,32768]{1,0:T(8,128)} %expert_pick.1), custom_call_target="tpu_custom_call" | custom-call | tf_op jit(solution)/shard_map/route/pallas_call | solution.py:337
  71.0 2.8 %decode.1 = (f32[6,32768]{1,0:T(8,128)}, f32[1,32768]{1,0:T(1,128)}, f32[3]{0:T(128)}) custom-call(s32[32,2,4,512]{3,2,1,0:T(4,128)S(1)} %get-tuple-element.5.recv_msg, f32[1,128]{1,0:T(1,128)S(1)} %get-tuple-element.6.sums), custom_call_target="tpu_custom_call" | custom-call | tf_op jit(solution)/shard_map/decode/pallas_call | solution.py:380
Async XLA Ops:
  0.6 0.9 %copy-start = (bf16[5120,5]{0,1:T(8,128)(2,1)S(1)}, bf16[5120,5]{0,1:T(8,128)(2,1)}, u32[]{:S(2)}) copy-start(bf16[5120,5]{0,1:T(8,128)(2,1)} %param.5) | copy-start | bytes 153604
where the time goes:
time: 73.9 us; the launch traced here: 73.8 us
  Pallas kernels  72.3 us (98%)
  local copies, waits for them, and re-layouts  0.88 us (1%)
    pallas_call x1, Pallas kernels, local(): pl.pallas_call(functools.partial(kernel, (ndp, ndev, per_dev, width, chun...  69.5 us
    pallas_call x1, Pallas kernels, local(): pl.pallas_call(functools.partial(decode, (ndev, share, width, chunks)), o...  2.77 us

commit v1 on v0

v1 whole, which is shorter than its diff:
```python
import jax
import jax.numpy as jnp
from jax import lax
from jax.experimental import pallas as pl
from jax.experimental.pallas import tpu as pltpu
from jax.sharding import PartitionSpec as P

MESH = pl.DeviceIdType.MESH
TOP = 6
DEV_TOP = 3
PER = 5
NX, NZ, NY = 4, 8, 4
NDP = 2 * NX
NDEV = NZ * NY
CODE = 1.4426950408889634 * 2048.0
NEG = -1e30
WORDS = TOP // 2
CHUNKS = 2
Z_ORDER = (1, 7, 2, 6, 3, 5, 4)
Y_ORDER = (1, 3, 2)


def rem(a, b):
    return lax.rem(a, b)


def encode(log_norm, value):
    return jnp.clip((log_norm - value) * CODE + 0.5, 0.0, 65535.0).astype(jnp.int32)


def low_half(words):
    return jnp.exp2((words & 65535).astype(jnp.float32) * (-1.0 / 2048.0))


def high_half(words):
    return jnp.exp2(lax.shift_right_logical(words, 16).astype(jnp.float32) * (-1.0 / 2048.0))


def kernel(
    tokens, router, device_pick, expert_pick,
    gates, device_max, balance,
    tok, raw, picks, dpicks, main, tail, lhs, part, prob_acc, top_code, gate_msg, top_msg, top_recv,
    cnt_dp, cnt_all, bal_dp, bal_z, bal_y,
    in_sem, tok_sem, zs, zr, ys, yr, cs, cr, ks, kr, gzs, gzr, gys, gyr, ts, tr, bs, br,
):
    depth, share = tokens.shape
    half, width = depth // 2, share // CHUNKS
    quarter = depth // 4
    total = share * NDEV * NDP
    dp, me = lax.axis_index("dp"), lax.axis_index("expert")
    core, z, y = rem(dp, 2), me // NY, rem(me, NY)
    partner = dp + 1 - 2 * core

    def zz(j):
        return rem(z + NZ - j, NZ)

    def yy(q):
        return rem(y + NY - q, NY)

    def z_peer(j):
        return (dp, rem(z + j, NZ) * NY + y)

    def y_peer(q):
        return (dp, z * NY + rem(y + q, NY))

    def dp_peer(i):
        return (rem(dp + i, NDP), me)

    def send(src, dst, s, r, device):
        return pltpu.make_async_remote_copy(
            src_ref=src, dst_ref=dst, send_sem=s, recv_sem=r, device_id=device, device_id_type=MESH
        )

    raw_copy = pltpu.make_async_copy(router, raw, in_sem.at[0])
    pick_copy = pltpu.make_async_copy(expert_pick, picks, in_sem.at[1])
    dpick_copy = pltpu.make_async_copy(device_pick, dpicks, in_sem.at[2])
    raw_copy.start()
    pick_copy.start()
    dpick_copy.start()

    def token_copy(c):
        return pltpu.make_async_copy(tokens.at[:, pl.ds(c * width, width)], tok.at[c], tok_sem.at[c])

    for c in range(CHUNKS):
        token_copy(c).start()

    barrier = pltpu.get_barrier_semaphore()
    friends = [z_peer(j) for j in Z_ORDER] + [y_peer(q) for q in Y_ORDER] + [dp_peer(i) for i in range(1, NDP)]
    for device in friends:
        pl.semaphore_signal(barrier, inc=1, device_id=device, device_id_type=MESH)

    def tail_slot(zi, yi):
        return zi * NY + rem(yi, 2) * 2 + yi // 2

    raw_copy.wait()
    main[me] = raw[0:4, :]
    last = raw[4:5, :].astype(jnp.float32)
    tail[tail_slot(z, y)] = jnp.concatenate(
        [
            jnp.concatenate([last[:, 0:quarter], last[:, 2 * quarter : 3 * quarter]], axis=1),
            jnp.concatenate([last[:, quarter : 2 * quarter], last[:, 3 * quarter :]], axis=1),
        ],
        axis=0,
    ).astype(jnp.bfloat16)

    pick_copy.wait()
    dpick_copy.wait()
    one, nil = jnp.float32(1.0), jnp.float32(0.0)

    def count(i, carry):
        counts, sends = carry
        counts = list(counts)
        for b in range(8):
            cols = pl.ds(pl.multiple_of(i * 1024 + b * 128, 128), 128)
            seen = picks[:, cols] - me * PER
            for e in range(PER):
                counts[e] = counts[e] + jnp.where(seen == e, one, nil)
            sends = sends + jnp.where(dpicks[:, cols] == me, one, nil)
        return tuple(counts), sends

    counts, sends = lax.fori_loop(
        0,
        share * NDEV // 1024,
        count,
        (tuple(jnp.zeros((TOP, 128), jnp.float32) for _ in range(PER)), jnp.zeros((DEV_TOP, 128), jnp.float32)),
    )
    lane = lax.broadcasted_iota(jnp.int32, (1, 128), 1)

    def whole(v):
        return jnp.sum(jnp.sum(v, axis=0, keepdims=True), axis=1, keepdims=True)

    mine = jnp.where(lane == PER, whole(sends), nil)
    for e in range(PER):
        mine = jnp.where(lane == e, whole(counts[e]), mine)
    cnt_dp[dp] = mine

    pl.semaphore_wait(barrier, len(friends))

    def main_at(zi, yi, c):
        return main.at[zi * NY + yi, :, pl.ds(pl.multiple_of(c * half, half), half)]

    def tail_at(zi, yi, c):
        return tail.at[tail_slot(zi, yi), :, pl.ds(pl.multiple_of(c * quarter, quarter), quarter)]

    def z_copies(j, mine=True):
        zi = z if mine else zz(j)
        return [
            send(f(zi, y, core), f(zi, y, core), zs.at[n, j], zr.at[n, j], z_peer(j))
            for n, f in enumerate((main_at, tail_at))
        ]

    def y_copies(q, j, mine=True):
        yi = y if mine else yy(q)
        return [
            send(f(zz(j), yi, core), f(zz(j), yi, core), ys.at[n, q, j], yr.at[n, q, j], y_peer(q))
            for n, f in enumerate((main_at, tail_at))
        ]

    def core_copies(q, j, c):
        return [
            send(f(zz(j), yy(q), c), f(zz(j), yy(q), c), cs.at[n, q, j], cr.at[n, q, j], (partner, me))
            for n, f in enumerate((main_at, tail_at))
        ]

    def start(copies):
        for copy in copies:
            copy.start()

    def arrive(copies):
        for copy in copies:
            copy.wait_recv()

    for j in Z_ORDER:
        start(z_copies(j))
    for q in Y_ORDER:
        start(y_copies(q, 0))
    cnt_copies = [send(cnt_dp.at[dp], cnt_dp.at[dp], ks.at[0, i], kr.at[0, i], dp_peer(i)) for i in range(1, NDP)]
    start(cnt_copies)
    for j in Z_ORDER:
        arrive(z_copies(j, False))
        for q in Y_ORDER:
            start(y_copies(q, j))
        start(core_copies(0, j, core))

    arrive(cnt_copies)
    cnt_all[y, z] = jnp.sum(cnt_dp[...], axis=0)
    for q in Y_ORDER:
        arrive(y_copies(q, 0, False))
        start(core_copies(q, 0, core))
    cnt_z = [send(cnt_all.at[y, z], cnt_all.at[y, z], ks.at[1, j], kr.at[1, j], z_peer(j)) for j in range(1, NZ)]
    start(cnt_z)
    for n, j in enumerate(Z_ORDER):
        for q in Y_ORDER:
            arrive(y_copies(q, j, False))
            start(core_copies(q, j, core))
        if n == 4:
            arrive([send(cnt_all.at[y, zz(j)], cnt_all.at[y, zz(j)], ks.at[1, j], kr.at[1, j], z_peer(j)) for j in range(1, NZ)])
            cnt_y = [send(cnt_all.at[y], cnt_all.at[y], ks.at[2, q], kr.at[2, q], y_peer(q)) for q in Y_ORDER]
            start(cnt_y)
    for j in (0,) + Z_ORDER:
        for q in (0,) + Y_ORDER:
            if j or q:
                arrive(core_copies(q, j, 1 - core))

    block = 512
    for i in range(depth // block):
        lhs[0 : 4 * NDEV, i * block : (i + 1) * block] = main[:, :, i * block : (i + 1) * block].reshape(4 * NDEV, block)
    for h in range(2):
        for i in range(quarter // 256):
            piece = tail[:, :, h * quarter + i * 256 : h * quarter + (i + 1) * 256].reshape(2 * NDEV, 256)
            for s in range(2):
                at = (2 * h + s) * quarter + i * 256
                lhs[4 * NDEV :, at : at + 256] = piece

    row = lax.broadcasted_iota(jnp.int32, (4 * NDEV, 128), 0)
    ids = (row // 4) * PER + rem(row, 4)
    trow = lax.broadcasted_iota(jnp.int32, (2 * NDEV, 128), 0)
    tdev = (trow // 8) * NY + rem(trow // 2, 2) * 2 + rem(trow // 4, 2)
    even = rem(trow, 2) == 0
    tail_ids = jnp.where(even, tdev * PER + PER - 1, -1)
    row8 = lax.broadcasted_iota(jnp.int32, (NZ, 8, 128), 1)
    prob_acc[...] = jnp.zeros((6 * NDEV, 128), jnp.float32)

    def gate_at(src, c):
        return gate_msg.at[src, c]

    def gate_z(j, c, mine=True):
        src = me if mine else zz(j) * NY + y
        return send(gate_at(src, c), gate_at(src, c), gzs.at[j, c], gzr.at[j, c], z_peer(j))

    def gate_y(q, j, c, mine=True):
        src = zz(j) * NY + (y if mine else yy(q))
        return send(gate_at(src, c), gate_at(src, c), gys.at[q, j, c], gyr.at[q, j, c], y_peer(q))

    for c in range(CHUNKS):
        token_copy(c).wait()
        dots = [
            jnp.dot(
                lhs[:, s * quarter : (s + 1) * quarter],
                tok[c, s * quarter : (s + 1) * quarter, :],
                preferred_element_type=jnp.float32,
            )
            for s in range(4)
        ]
        split = 4 * NDEV
        part[0:split, :] = (dots[0][:split] + dots[1][:split]) + (dots[2][:split] + dots[3][:split])
        part[split : split + 2 * NDEV, :] = dots[0][split:] + dots[2][split:]
        part[split + 2 * NDEV :, :] = dots[1][split:] + dots[3][split:]
        for b in range(width // 128):
            cols = slice(b * 128, (b + 1) * 128)
            scores = part[0:split, cols]
            mixed = jnp.where(even, part[split : split + 2 * NDEV, cols], part[split + 2 * NDEV :, cols])
            mixed = mixed.reshape(NZ, 8, 128)
            mixed = (mixed + pltpu.roll(mixed, 7, axis=1)).reshape(2 * NDEV, 128)
            last = jnp.where(even, mixed, NEG)
            peak = jnp.maximum(jnp.max(scores, axis=0, keepdims=True), jnp.max(last, axis=0, keepdims=True))
            scores = scores - peak
            last = jnp.where(even, last - peak, NEG)
            raised = jnp.exp(scores)
            raised_last = jnp.exp(last)
            norm = jnp.sum(raised, axis=0, keepdims=True) + jnp.sum(raised_last, axis=0, keepdims=True)
            inverse = 1.0 / norm
            prob_acc[0:split, :] += raised * inverse
            prob_acc[split:, :] += raised_last * inverse
            log_norm = jnp.log(norm)
            at = pl.ds(pl.multiple_of(me * share + c * width + b * 128, 128), 128)
            codes = []
            for k in range(TOP):
                pick = picks[k : k + 1, at]
                found = jnp.max(jnp.where(pick == ids, scores, NEG), axis=0, keepdims=True)
                found_last = jnp.max(jnp.where(pick == tail_ids, last, NEG), axis=0, keepdims=True)
                codes.append(encode(log_norm, jnp.maximum(found, found_last)))
            for w in range(WORDS):
                gate_msg[me, c, w, b : b + 1, :] = codes[w] + jnp.left_shift(codes[w + WORDS], 16)
            best = scores.reshape(2 * NZ, 8, 128)
            best = jnp.maximum(best, pltpu.roll(best, 7, axis=1))
            best = jnp.maximum(best, pltpu.roll(best, 6, axis=1)).reshape(NZ, 2, 8, 128)
            best = jnp.where(rem(row8, 4) < 2, best[:, 0], pltpu.roll(best[:, 1], 2, axis=1))
            best = jnp.maximum(best, last.reshape(NZ, 8, 128))
            code = encode(log_norm.reshape(1, 1, 128), best)
            if c == 0:
                top_code[:, :, cols] = code
            else:
                words = top_code[:, :, cols] + jnp.left_shift(code, 16)
                for zi in range(NZ):
                    for yi in range(NY):
                        r = 2 * ((yi % 2) * 2 + yi // 2)
                        top_msg[zi * NY + yi, :, cols] = words[zi, r : r + 1, :]
        for j in Z_ORDER:
            gate_z(j, c).start()
        for q in Y_ORDER:
            gate_y(q, 0, c).start()

    def top_copy(i):
        return send(top_msg.at[rem(me + i, NDEV)], top_recv.at[me], ts.at[i], tr.at[i], (dp, rem(me + i, NDEV)))

    def start_top(i, carry):
        top_copy(i).start()
        return carry

    lax.fori_loop(1, NDEV, start_top, 0)
    top_recv[me] = top_msg[me]

    arrive([send(cnt_all.at[yy(q)], cnt_all.at[yy(q)], ks.at[2, q], kr.at[2, q], y_peer(q)) for q in Y_ORDER])
    sums = [jnp.float32(0.0)] * 3
    dev_prob, dev_count, sent = [nil] * NY, [nil] * NY, [nil] * NY
    acc = [jnp.zeros((NZ, 128), jnp.float32)] * 3
    for yi in range(NY):
        table = cnt_all[yi].reshape(NZ, 128)
        lanes = lax.broadcasted_iota(jnp.int32, (NZ, 128), 1)
        dev_prob = jnp.zeros((NZ, 128), jnp.float32)
        dev_count = jnp.zeros((NZ, 1), jnp.float32)
        for e in range(PER):
            cnt = jnp.sum(jnp.where(lanes == e, table, nil), axis=1, keepdims=True)
            if e < PER - 1:
                prob = prob_acc[pl.ds(yi * 4 + e, NZ, stride=16), :]
            else:
                prob = prob_acc[pl.ds(4 * NDEV + 2 * ((yi % 2) * 2 + yi // 2), NZ, stride=8), :]
            acc[0] = acc[0] + prob * cnt
            dev_prob = dev_prob + prob
            dev_count = dev_count + cnt
        acc[1] = acc[1] + dev_prob * dev_count
        acc[2] = acc[2] + dev_prob * jnp.sum(jnp.where(lanes == PER, table, nil), axis=1, keepdims=True)
    experts = NDEV * PER
    scale = (experts / (TOP * total) / total, experts / (TOP * total) / PER / total, NDEV / (DEV_TOP * total) / total)
    result = jnp.zeros((1, 128), jnp.float32)
    for i in range(3):
        result = jnp.where(lane == i, whole(acc[i]) * scale[i], result)
    bal_dp[dp] = result
    bal_copies = [send(bal_dp.at[dp], bal_dp.at[dp], bs.at[0, i], br.at[0, i], dp_peer(i)) for i in range(1, NDP)]
    start(bal_copies)

    def show(src, c):
        words = gate_msg[src, c]
        low, high = low_half(words), high_half(words)
        for b in range(width // 128):
            cols = pl.ds(pl.multiple_of(src * share + c * width + b * 128, 128), 128)
            gates[0:WORDS, cols] = low[:, b, :]
            gates[WORDS:TOP, cols] = high[:, b, :]

    for c in range(CHUNKS):
        for j in Z_ORDER:
            gate_z(j, c, False).wait_recv()
            for q in Y_ORDER:
                gate_y(q, j, c).start()
    arrive(bal_copies)
    bal_z[z] = jnp.sum(bal_dp[...], axis=0)
    bal_zs = [send(bal_z.at[z], bal_z.at[z], bs.at[1, j], br.at[1, j], z_peer(j)) for j in range(1, NZ)]
    start(bal_zs)
    for c in range(CHUNKS):
        for j in (0,) + Z_ORDER:
            show(zz(j) * NY + y, c)
    arrive(bal_zs)
    bal_y[y] = jnp.sum(bal_z[...], axis=0)
    bal_ys = [send(bal_y.at[y], bal_y.at[y], bs.at[2, q], br.at[2, q], y_peer(q)) for q in Y_ORDER]
    start(bal_ys)
    for c in range(CHUNKS):
        for j in (0,) + Z_ORDER:
            for q in Y_ORDER:
                gate_y(q, j, c, False).wait_recv()
                show(zz(j) * NY + yy(q), c)

    def show_top(i, carry):
        src = rem(me + NDEV - i, NDEV)

        @pl.when(i > 0)
        def _():
            top_copy(i).wait_recv()

        words = top_recv[src]
        device_max[:, pl.ds(pl.multiple_of(src * share, share), width)] = low_half(words)
        device_max[:, pl.ds(pl.multiple_of(src * share + width, width), width)] = high_half(words)
        return carry

    lax.fori_loop(0, NDEV, show_top, 0)
    arrive(bal_ys)
    balance[...] = jnp.sum(bal_y[...], axis=0)

    for j in Z_ORDER:
        for copy in z_copies(j):
            copy.wait_send()
        for c in range(CHUNKS):
            gate_z(j, c).wait_send()
    for j in (0,) + Z_ORDER:
        for q in Y_ORDER:
            for copy in y_copies(q, j):
                copy.wait_send()
            for c in range(CHUNKS):
                gate_y(q, j, c).wait_send()
        for q in (0,) + Y_ORDER:
            if j or q:
                for copy in core_copies(q, j, core):
                    copy.wait_send()
    for copy in cnt_copies + cnt_z + cnt_y + bal_copies + bal_zs + bal_ys:
        copy.wait_send()

    def sent_top(i, carry):
        top_copy(i).wait_send()
        return carry

    lax.fori_loop(1, NDEV, sent_top, 0)


def put(gate_buf, top_buf, sums, gates, device_max, balance, sem):
    first = pltpu.make_async_copy(gate_buf, gates, sem.at[0])
    second = pltpu.make_async_copy(top_buf, device_max, sem.at[1])
    first.start()
    second.start()
    lane = lax.broadcasted_iota(jnp.int32, (1, 128), 1)
    for i in range(3):
        balance[i] = jnp.sum(jnp.where(lane == i, sums[...], jnp.float32(0.0)))
    first.wait()
    second.wait()


def local(tokens, router, device_pick, expert_pick):
    depth, share = tokens.shape
    width = share // CHUNKS
    dma = pltpu.SemaphoreType.DMA
    f32, i32, bf16 = jnp.float32, jnp.int32, jnp.bfloat16
    outs = (
        jax.ShapeDtypeStruct((TOP, share * NDEV), f32),
        jax.ShapeDtypeStruct((1, share * NDEV), f32),
        jax.ShapeDtypeStruct((1, 128), f32),
    )
    buffers = pl.pallas_call(
        kernel,
        out_shape=outs,
        in_specs=[pl.BlockSpec(memory_space=pltpu.HBM)] * 4,
        out_specs=tuple(pl.BlockSpec(memory_space=pltpu.VMEM) for _ in outs),
        scratch_shapes=[
            pltpu.VMEM((CHUNKS, depth, width), bf16),
            pltpu.VMEM((PER, depth), bf16),
            pltpu.VMEM((TOP, share * NDEV), i32),
            pltpu.VMEM((DEV_TOP, share * NDEV), i32),
            pltpu.VMEM((NDEV, 4, depth), bf16),
            pltpu.VMEM((NDEV, 2, depth // 2), bf16),
            pltpu.VMEM((6 * NDEV, depth), bf16),
            pltpu.VMEM((8 * NDEV, width), f32),
            pltpu.VMEM((6 * NDEV, 128), f32),
            pltpu.VMEM((NZ, 8, width), i32),
            pltpu.VMEM((NDEV, CHUNKS, WORDS, width // 128, 128), i32),
            pltpu.VMEM((NDEV, 1, width), i32),
            pltpu.VMEM((NDEV, 1, width), i32),
            pltpu.VMEM((NDP, 1, 128), f32),
            pltpu.VMEM((NY, NZ, 1, 128), f32),
            pltpu.VMEM((NDP, 1, 128), f32),
            pltpu.VMEM((NZ, 1, 128), f32),
            pltpu.VMEM((NY, 1, 128), f32),
            dma((3,)),
            dma((CHUNKS,)),
            dma((2, NZ)),
            dma((2, NZ)),
            dma((2, NY, NZ)),
            dma((2, NY, NZ)),
            dma((2, NY, NZ)),
            dma((2, NY, NZ)),
            dma((3, NZ)),
            dma((3, NZ)),
            dma((NZ, CHUNKS)),
            dma((NZ, CHUNKS)),
            dma((NY, NZ, CHUNKS)),
            dma((NY, NZ, CHUNKS)),
            dma((NDEV,)),
            dma((NDEV,)),
            dma((3, NZ)),
            dma((3, NZ)),
        ],
        compiler_params=pltpu.CompilerParams(
            collective_id=0, has_side_effects=True, vmem_limit_bytes=62 * 1024 * 1024
        ),
        name="route",
    )(tokens, router.T, device_pick, expert_pick)
    return pl.pallas_call(
        put,
        out_shape=outs[:2] + (jax.ShapeDtypeStruct((3,), f32),),
        in_specs=[pl.BlockSpec(memory_space=pltpu.VMEM)] * 3,
        out_specs=(
            pl.BlockSpec(memory_space=pl.ANY),
            pl.BlockSpec(memory_space=pl.ANY),
            pl.BlockSpec(memory_space=pltpu.SMEM),
        ),
        scratch_shapes=[dma((2,))],
        compiler_params=pltpu.CompilerParams(vmem_limit_bytes=8 * 1024 * 1024),
        name="put",
    )(*buffers)


def solution(mesh):
    placed = (P(None, ("dp", "expert")), P(None, "expert"), P(None, "dp"), P(None, "dp"))
    return jax.shard_map(
        local,
        mesh=mesh,
        in_specs=placed,
        out_specs=(P(None, "dp"), P("expert", "dp"), P()),
        check_vma=False,
    )
```

time: 73.9 us -> 51.2 us (0.69)
  Pallas kernels: 72.3 us -> 47.7 us
  local copies, waits for them, and re-layouts: 0.88 us -> 2.72 us
    pallas_call x2, Pallas kernels: 72.3 us -> 47.7 us  [the longest x1 46.2 us: local(): pl.pallas_call(kernel, out_shape=outs, in_specs=[pl.BlockSpec(memory_spac...]
    unnamed x2 -> x6, local copies, waits for them, and re-layouts: 0.88 us -> 2.72 us
where the time goes in v1:
time: 51.2 us; the launch traced here: 51.1 us
  Pallas kernels  47.7 us (93%)
  local copies, waits for them, and re-layouts  2.72 us (5%)
  between operations  0.65 us (1%)
    pallas_call x1, Pallas kernels, local(): pl.pallas_call(kernel, out_shape=outs, in_specs=[pl.BlockSpec(memory_spac...  46.2 us
    unnamed x6, local copies, waits for them, and re-layouts  2.72 us
    pallas_call x1, Pallas kernels, local(): pl.pallas_call(put, out_shape=outs[:2] + (jax.ShapeDtypeStruct((3,), f32)...  1.53 us

profile of v1, /device:TPU:1, one launch (start us, length us, event | category | flops | bytes accessed | tf_op | source)
XLA Modules:
  0.0 51.1 jit_solution(16309965376070749039)
XLA Ops:
  0.6 46.2 %route.1 = (f32[6,32768]{1,0:T(8,128)}, f32[1,32768]{1,0:T(1,128)}, f32[1,128]{1,0:T(1,128)}) custom-call(bf16[5120,1024]{1,0:T(8,128)(2,1)} %tokens.1, bf16[5,5120]{1,0:T(8,128)(2,1)} %bitcast.1, s32[3,32768]{1,0:T(4,128)} %device_pick.1, s32[6,32768]{1,0:T(8,128)} %expert_pick.1), custom_call_target="tpu_custom_call" | custom-call | tf_op jit(solution)/shard_map/route/pallas_call | solution.py:426
  46.8 0.0 copy-start
  46.8 1.2 %copy-done = f32[6,32768]{1,0:T(8,128)S(1)} copy-done((f32[6,32768]{1,0:T(8,128)S(1)}, f32[6,32768]{1,0:T(8,128)}, u32[]{:S(2)}) %copy-start) | copy-done | bytes 786456
  48.1 0.0 copy-start.1
  48.1 0.9 %copy-done.1 = f32[1,32768]{1,0:T(1,128)S(1)} copy-done((f32[1,32768]{1,0:T(1,128)S(1)}, f32[1,32768]{1,0:T(1,128)}, u32[]{:S(2)}) %copy-start.1) | copy-done | bytes 131096
  49.0 0.0 copy-start.2
  49.0 0.6 %copy-done.2 = f32[1,128]{1,0:T(1,128)S(1)} copy-done((f32[1,128]{1,0:T(1,128)S(1)}, f32[1,128]{1,0:T(1,128)}, u32[]{:S(2)}) %copy-start.2) | copy-done | bytes 536
  49.6 1.5 %put.1 = (f32[6,32768]{1,0:T(8,128)}, f32[1,32768]{1,0:T(1,128)}, f32[3]{0:T(128)}) custom-call(f32[6,32768]{1,0:T(8,128)S(1)} %copy-done, f32[1,32768]{1,0:T(1,128)S(1)} %copy-done.1, f32[1,128]{1,0:T(1,128)S(1)} %copy-done.2), custom_call_target="tpu_custom_call" | custom-call | tf_op jit(solution)/shard_map/put/pallas_call | solution.py:474
Async XLA Ops:
  46.8 1.2 %copy-start = (f32[6,32768]{1,0:T(8,128)S(1)}, f32[6,32768]{1,0:T(8,128)}, u32[]{:S(2)}) copy-start(f32[6,32768]{1,0:T(8,128)} %get-tuple-element.6.gate_buf) | copy-start | bytes 2359300
  48.1 0.9 %copy-start.1 = (f32[1,32768]{1,0:T(1,128)S(1)}, f32[1,32768]{1,0:T(1,128)}, u32[]{:S(2)}) copy-start(f32[1,32768]{1,0:T(1,128)} %get-tuple-element.7.top_buf) | copy-start | bytes 393220
  49.0 0.6 %copy-start.2 = (f32[1,128]{1,0:T(1,128)S(1)}, f32[1,128]{1,0:T(1,128)}, u32[]{:S(2)}) copy-start(f32[1,128]{1,0:T(1,128)} %get-tuple-element.8.sums) | copy-start | bytes 1540

commit v2 on v1

--- a/solution.py
+++ b/solution.py
@@ -16,6 +16,7 @@
 NEG = -1e30
 WORDS = TOP // 2
 CHUNKS = 2
+VMEM = 67043328
 Z_ORDER = (1, 7, 2, 6, 3, 5, 4)
 Y_ORDER = (1, 3, 2)
 
@@ -37,10 +38,10 @@
 
 
 def kernel(
-    tokens, router, device_pick, expert_pick,
+    tokens, router, expert_pick,
     gates, device_max, balance,
-    tok, raw, picks, dpicks, main, tail, lhs, part, prob_acc, top_code, gate_msg, top_msg, top_recv,
-    cnt_dp, cnt_all, bal_dp, bal_z, bal_y,
+    tok, picks, main, tail, lhs, part, prob_acc, top_code, gate_msg, top_msg, top_recv,
+    cnt_dp, cnt_all, bal_plane, bal_dp,
     in_sem, tok_sem, zs, zr, ys, yr, cs, cr, ks, kr, gzs, gzr, gys, gyr, ts, tr, bs, br,
 ):
     depth, share = tokens.shape
@@ -71,12 +72,8 @@
             src_ref=src, dst_ref=dst, send_sem=s, recv_sem=r, device_id=device, device_id_type=MESH
         )
 
-    raw_copy = pltpu.make_async_copy(router, raw, in_sem.at[0])
-    pick_copy = pltpu.make_async_copy(expert_pick, picks, in_sem.at[1])
-    dpick_copy = pltpu.make_async_copy(device_pick, dpicks, in_sem.at[2])
-    raw_copy.start()
+    pick_copy = pltpu.make_async_copy(expert_pick, picks, in_sem.at[0])
     pick_copy.start()
-    dpick_copy.start()
 
     def token_copy(c):
         return pltpu.make_async_copy(tokens.at[:, pl.ds(c * width, width)], tok.at[c], tok_sem.at[c])
@@ -92,9 +89,8 @@
     def tail_slot(zi, yi):
         return zi * NY + rem(yi, 2) * 2 + yi // 2
 
-    raw_copy.wait()
-    main[me] = raw[0:4, :]
-    last = raw[4:5, :].astype(jnp.float32)
+    main[me] = router[0:4, :]
+    last = router[4:5, :].astype(jnp.float32)
     tail[tail_slot(z, y)] = jnp.concatenate(
         [
             jnp.concatenate([last[:, 0:quarter], last[:, 2 * quarter : 3 * quarter]], axis=1),
@@ -103,77 +99,70 @@
         axis=0,
     ).astype(jnp.bfloat16)
 
+    pl.semaphore_wait(barrier, len(friends))
+
+    def main_at(zi, yi, c):
+        return main.at[zi * NY + yi, :, pl.ds(pl.multiple_of(c * half, half), half)]
+
+    def tail_at(zi, yi, c):
+        return tail.at[tail_slot(zi, yi), :, pl.ds(pl.multiple_of(c * quarter, quarter), quarter)]
+
+    def z_copies(j, mine=True):
+        zi = z if mine else zz(j)
+        return [
+            send(f(zi, y, core), f(zi, y, core), zs.at[n, j], zr.at[n, j], z_peer(j))
+            for n, f in enumerate((main_at, tail_at))
+        ]
+
+    def y_copies(q, j, mine=True):
+        yi = y if mine else yy(q)
+        return [
+            send(f(zz(j), yi, core), f(zz(j), yi, core), ys.at[n, q, j], yr.at[n, q, j], y_peer(q))
+            for n, f in enumerate((main_at, tail_at))
+        ]
+
+    def core_copies(q, j, c):
+        return [
+            send(f(zz(j), yy(q), c), f(zz(j), yy(q), c), cs.at[n, q, j], cr.at[n, q, j], (partner, me))
+            for n, f in enumerate((main_at, tail_at))
+        ]
+
+    def start(copies):
+        for copy in copies:
+            copy.start()
+
+    def arrive(copies):
+        for copy in copies:
+            copy.wait_recv()
+
+    for j in Z_ORDER:
+        start(z_copies(j))
+    for q in Y_ORDER:
+        start(y_copies(q, 0))
     pick_copy.wait()
-    dpick_copy.wait()
     one, nil = jnp.float32(1.0), jnp.float32(0.0)
 
-    def count(i, carry):
-        counts, sends = carry
+    def count(i, counts):
         counts = list(counts)
         for b in range(8):
             cols = pl.ds(pl.multiple_of(i * 1024 + b * 128, 128), 128)
             seen = picks[:, cols] - me * PER
             for e in range(PER):
                 counts[e] = counts[e] + jnp.where(seen == e, one, nil)
-            sends = sends + jnp.where(dpicks[:, cols] == me, one, nil)
-        return tuple(counts), sends
-
-    counts, sends = lax.fori_loop(
-        0,
-        share * NDEV // 1024,
-        count,
-        (tuple(jnp.zeros((TOP, 128), jnp.float32) for _ in range(PER)), jnp.zeros((DEV_TOP, 128), jnp.float32)),
-    )
+        return tuple(counts)
+
+    nothing = tuple(jnp.zeros((TOP, 128), jnp.float32) for _ in range(PER))
+    counts = lax.fori_loop(0, share * NDEV // 1024, count, nothing)
     lane = lax.broadcasted_iota(jnp.int32, (1, 128), 1)
 
     def whole(v):
         return jnp.sum(jnp.sum(v, axis=0, keepdims=True), axis=1, keepdims=True)
 
-    mine = jnp.where(lane == PER, whole(sends), nil)
+    mine = jnp.zeros((1, 128), jnp.float32)
     for e in range(PER):
         mine = jnp.where(lane == e, whole(counts[e]), mine)
     cnt_dp[dp] = mine
 
-    pl.semaphore_wait(barrier, len(friends))
-
-    def main_at(zi, yi, c):
-        return main.at[zi * NY + yi, :, pl.ds(pl.multiple_of(c * half, half), half)]
-
-    def tail_at(zi, yi, c):
-        return tail.at[tail_slot(zi, yi), :, pl.ds(pl.multiple_of(c * quarter, quarter), quarter)]
-
-    def z_copies(j, mine=True):
-        zi = z if mine else zz(j)
-        return [
-            send(f(zi, y, core), f(zi, y, core), zs.at[n, j], zr.at[n, j], z_peer(j))
-            for n, f in enumerate((main_at, tail_at))
-        ]
-
-    def y_copies(q, j, mine=True):
-        yi = y if mine else yy(q)
-        return [
-            send(f(zz(j), yi, core), f(zz(j), yi, core), ys.at[n, q, j], yr.at[n, q, j], y_peer(q))
-            for n, f in enumerate((main_at, tail_at))
-        ]
-
-    def core_copies(q, j, c):
-        return [
-            send(f(zz(j), yy(q), c), f(zz(j), yy(q), c), cs.at[n, q, j], cr.at[n, q, j], (partner, me))
-            for n, f in enumerate((main_at, tail_at))
-        ]
-
-    def start(copies):
-        for copy in copies:
-            copy.start()
-
-    def arrive(copies):
-        for copy in copies:
-            copy.wait_recv()
-
-    for j in Z_ORDER:
-        start(z_copies(j))
-    for q in Y_ORDER:
-        start(y_copies(q, 0))
     cnt_copies = [send(cnt_dp.at[dp], cnt_dp.at[dp], ks.at[0, i], kr.at[0, i], dp_peer(i)) for i in range(1, NDP)]
     start(cnt_copies)
     for j in Z_ORDER:
@@ -197,20 +186,46 @@
             arrive([send(cnt_all.at[y, zz(j)], cnt_all.at[y, zz(j)], ks.at[1, j], kr.at[1, j], z_peer(j)) for j in range(1, NZ)])
             cnt_y = [send(cnt_all.at[y], cnt_all.at[y], ks.at[2, q], kr.at[2, q], y_peer(q)) for q in Y_ORDER]
             start(cnt_y)
+    split = 4 * NDEV
+    block = 512
+
+    def half_of(h):
+        return core if h == 0 else 1 - core
+
+    def gather_rows(h):
+        lanes = half_of(h) * half
+        for i in range(half // block):
+            piece = main[:, :, pl.ds(pl.multiple_of(lanes + i * block, 128), block)]
+            lhs[h, 0:split, i * block : (i + 1) * block] = piece.reshape(split, block)
+        lanes = half_of(h) * quarter
+        for i in range(quarter // 256):
+            piece = tail[:, :, pl.ds(pl.multiple_of(lanes + i * 256, 128), 256)].reshape(2 * NDEV, 256)
+            for s in range(2):
+                lhs[h, split:, s * quarter + i * 256 : s * quarter + (i + 1) * 256] = piece
+
+    def dots(h, c):
+        return [
+            jnp.dot(
+                lhs[h, :, s * quarter : (s + 1) * quarter],
+                tok[c, pl.ds(pl.multiple_of(half_of(h) * half + s * quarter, 128), quarter), :],
+                preferred_element_type=jnp.float32,
+            )
+            for s in range(2)
+        ]
+
+    gather_rows(0)
+    for c in range(CHUNKS):
+        token_copy(c).wait()
+        first, second = dots(0, c)
+        part[c, 0:split, :] = first[:split] + second[:split]
+        part[c, split : split + 2 * NDEV, :] = first[split:]
+        part[c, split + 2 * NDEV :, :] = second[split:]
+
     for j in (0,) + Z_ORDER:
         for q in (0,) + Y_ORDER:
             if j or q:
                 arrive(core_copies(q, j, 1 - core))
-
-    block = 512
-    for i in range(depth // block):
-        lhs[0 : 4 * NDEV, i * block : (i + 1) * block] = main[:, :, i * block : (i + 1) * block].reshape(4 * NDEV, block)
-    for h in range(2):
-        for i in range(quarter // 256):
-            piece = tail[:, :, h * quarter + i * 256 : h * quarter + (i + 1) * 256].reshape(2 * NDEV, 256)
-            for s in range(2):
-                at = (2 * h + s) * quarter + i * 256
-                lhs[4 * NDEV :, at : at + 256] = piece
+    gather_rows(1)
 
     row = lax.broadcasted_iota(jnp.int32, (4 * NDEV, 128), 0)
     ids = (row // 4) * PER + rem(row, 4)
@@ -233,23 +248,14 @@
         return send(gate_at(src, c), gate_at(src, c), gys.at[q, j, c], gyr.at[q, j, c], y_peer(q))
 
     for c in range(CHUNKS):
-        token_copy(c).wait()
-        dots = [
-            jnp.dot(
-                lhs[:, s * quarter : (s + 1) * quarter],
-                tok[c, s * quarter : (s + 1) * quarter, :],
-                preferred_element_type=jnp.float32,
-            )
-            for s in range(4)
-        ]
-        split = 4 * NDEV
-        part[0:split, :] = (dots[0][:split] + dots[1][:split]) + (dots[2][:split] + dots[3][:split])
-        part[split : split + 2 * NDEV, :] = dots[0][split:] + dots[2][split:]
-        part[split + 2 * NDEV :, :] = dots[1][split:] + dots[3][split:]
+        first, second = dots(1, c)
+        part[c, 0:split, :] += first[:split] + second[:split]
+        part[c, split : split + 2 * NDEV, :] += first[split:]
+        part[c, split + 2 * NDEV :, :] += second[split:]
         for b in range(width // 128):
             cols = slice(b * 128, (b + 1) * 128)
-            scores = part[0:split, cols]
-            mixed = jnp.where(even, part[split : split + 2 * NDEV, cols], part[split + 2 * NDEV :, cols])
+            scores = part[c, 0:split, cols]
+            mixed = jnp.where(even, part[c, split : split + 2 * NDEV, cols], part[c, split + 2 * NDEV :, cols])
             mixed = mixed.reshape(NZ, 8, 128)
             mixed = (mixed + pltpu.roll(mixed, 7, axis=1)).reshape(2 * NDEV, 128)
             last = jnp.where(even, mixed, NEG)
@@ -291,19 +297,7 @@
         for q in Y_ORDER:
             gate_y(q, 0, c).start()
 
-    def top_copy(i):
-        return send(top_msg.at[rem(me + i, NDEV)], top_recv.at[me], ts.at[i], tr.at[i], (dp, rem(me + i, NDEV)))
-
-    def start_top(i, carry):
-        top_copy(i).start()
-        return carry
-
-    lax.fori_loop(1, NDEV, start_top, 0)
-    top_recv[me] = top_msg[me]
-
     arrive([send(cnt_all.at[yy(q)], cnt_all.at[yy(q)], ks.at[2, q], kr.at[2, q], y_peer(q)) for q in Y_ORDER])
-    sums = [jnp.float32(0.0)] * 3
-    dev_prob, dev_count, sent = [nil] * NY, [nil] * NY, [nil] * NY
     acc = [jnp.zeros((NZ, 128), jnp.float32)] * 3
     for yi in range(NY):
         table = cnt_all[yi].reshape(NZ, 128)
@@ -320,15 +314,32 @@
             dev_prob = dev_prob + prob
             dev_count = dev_count + cnt
         acc[1] = acc[1] + dev_prob * dev_count
-        acc[2] = acc[2] + dev_prob * jnp.sum(jnp.where(lanes == PER, table, nil), axis=1, keepdims=True)
+        acc[2] = acc[2] + dev_prob * (dev_count * 0.5)
     experts = NDEV * PER
     scale = (experts / (TOP * total) / total, experts / (TOP * total) / PER / total, NDEV / (DEV_TOP * total) / total)
     result = jnp.zeros((1, 128), jnp.float32)
     for i in range(3):
         result = jnp.where(lane == i, whole(acc[i]) * scale[i], result)
-    bal_dp[dp] = result
-    bal_copies = [send(bal_dp.at[dp], bal_dp.at[dp], bs.at[0, i], br.at[0, i], dp_peer(i)) for i in range(1, NDP)]
-    start(bal_copies)
+    bal_plane[me] = result
+
+    def plane_copy(i):
+        return send(bal_plane.at[me], bal_plane.at[me], bs.at[0, i], br.at[0, i], (dp, rem(me + i, NDEV)))
+
+    def start_plane(i, carry):
+        plane_copy(i).start()
+        return carry
+
+    lax.fori_loop(1, NDEV, start_plane, 0)
+
+    def top_copy(i):
+        return send(top_msg.at[rem(me + i, NDEV)], top_recv.at[me], ts.at[i], tr.at[i], (dp, rem(me + i, NDEV)))
+
+    def start_top(i, carry):
+        top_copy(i).start()
+        return carry
+
+    lax.fori_loop(1, NDEV, start_top, 0)
+    top_recv[me] = top_msg[me]
 
     def show(src, c):
         words = gate_msg[src, c]
@@ -343,17 +354,26 @@
             gate_z(j, c, False).wait_recv()
             for q in Y_ORDER:
                 gate_y(q, j, c).start()
-    arrive(bal_copies)
-    bal_z[z] = jnp.sum(bal_dp[...], axis=0)
-    bal_zs = [send(bal_z.at[z], bal_z.at[z], bs.at[1, j], br.at[1, j], z_peer(j)) for j in range(1, NZ)]
-    start(bal_zs)
     for c in range(CHUNKS):
         for j in (0,) + Z_ORDER:
             show(zz(j) * NY + y, c)
-    arrive(bal_zs)
-    bal_y[y] = jnp.sum(bal_z[...], axis=0)
-    bal_ys = [send(bal_y.at[y], bal_y.at[y], bs.at[2, q], br.at[2, q], y_peer(q)) for q in Y_ORDER]
-    start(bal_ys)
+
+    def take_plane(i, carry):
+        plane_copy(i).wait_recv()
+        return carry
+
+    lax.fori_loop(1, NDEV, take_plane, 0)
+    bal_dp[dp] = jnp.sum(bal_plane[...], axis=0)
+    bal_copies = [send(bal_dp.at[dp], bal_dp.at[dp], bs.at[1, i], br.at[1, i], dp_peer(i)) for i in range(1, NDP)]
+    start(bal_copies)
+    for j in (0,) + Z_ORDER:
+        for copy in z_copies(j) if j else ():
+            copy.wait_send()
+        for q in (0,) + Y_ORDER:
+            for copy in (y_copies(q, j) if q else []) + (core_copies(q, j, core) if j or q else []):
+                copy.wait_send()
+    for copy in cnt_copies + cnt_z + cnt_y:
+        copy.wait_send()
     for c in range(CHUNKS):
         for j in (0,) + Z_ORDER:
             for q in Y_ORDER:
@@ -373,29 +393,21 @@
         return carry
 
     lax.fori_loop(0, NDEV, show_top, 0)
-    arrive(bal_ys)
-    balance[...] = jnp.sum(bal_y[...], axis=0)
-
-    for j in Z_ORDER:
-        for copy in z_copies(j):
-            copy.wait_send()
+    arrive(bal_copies)
+    balance[...] = jnp.sum(bal_dp[...], axis=0)
+
+    for j in (0,) + Z_ORDER:
         for c in range(CHUNKS):
-            gate_z(j, c).wait_send()
-    for j in (0,) + Z_ORDER:
-        for q in Y_ORDER:
-            for copy in y_copies(q, j):
-                copy.wait_send()
-            for c in range(CHUNKS):
+            if j:
+                gate_z(j, c).wait_send()
+            for q in Y_ORDER:
                 gate_y(q, j, c).wait_send()
-        for q in (0,) + Y_ORDER:
-            if j or q:
-                for copy in core_copies(q, j, core):
-                    copy.wait_send()
-    for copy in cnt_copies + cnt_z + cnt_y + bal_copies + bal_zs + bal_ys:
+    for copy in bal_copies:
         copy.wait_send()
 
     def sent_top(i, carry):
         top_copy(i).wait_send()
+        plane_copy(i).wait_send()
         return carry
 
     lax.fori_loop(1, NDEV, sent_top, 0)
@@ -426,17 +438,15 @@
     buffers = pl.pallas_call(
         kernel,
         out_shape=outs,
-        in_specs=[pl.BlockSpec(memory_space=pltpu.HBM)] * 4,
+        in_specs=[pl.BlockSpec(memory_space=s) for s in (pltpu.HBM, pltpu.VMEM, pltpu.HBM)],
         out_specs=tuple(pl.BlockSpec(memory_space=pltpu.VMEM) for _ in outs),
         scratch_shapes=[
             pltpu.VMEM((CHUNKS, depth, width), bf16),
-            pltpu.VMEM((PER, depth), bf16),
             pltpu.VMEM((TOP, share * NDEV), i32),
-            pltpu.VMEM((DEV_TOP, share * NDEV), i32),
             pltpu.VMEM((NDEV, 4, depth), bf16),
             pltpu.VMEM((NDEV, 2, depth // 2), bf16),
-            pltpu.VMEM((6 * NDEV, depth), bf16),
-            pltpu.VMEM((8 * NDEV, width), f32),
+            pltpu.VMEM((2, 6 * NDEV, depth // 2), bf16),
+            pltpu.VMEM((CHUNKS, 8 * NDEV, width), f32),
             pltpu.VMEM((6 * NDEV, 128), f32),
             pltpu.VMEM((NZ, 8, width), i32),
             pltpu.VMEM((NDEV, CHUNKS, WORDS, width // 128, 128), i32),
@@ -444,10 +454,9 @@
             pltpu.VMEM((NDEV, 1, width), i32),
             pltpu.VMEM((NDP, 1, 128), f32),
             pltpu.VMEM((NY, NZ, 1, 128), f32),
+            pltpu.VMEM((NDEV, 1, 128), f32),
             pltpu.VMEM((NDP, 1, 128), f32),
-            pltpu.VMEM((NZ, 1, 128), f32),
-            pltpu.VMEM((NY, 1, 128), f32),
-            dma((3,)),
+            dma((1,)),
             dma((CHUNKS,)),
             dma((2, NZ)),
             dma((2, NZ)),
@@ -463,14 +472,14 @@
             dma((NY, NZ, CHUNKS)),
             dma((NDEV,)),
             dma((NDEV,)),
-            dma((3, NZ)),
-            dma((3, NZ)),
+            dma((2, NDEV)),
+            dma((2, NDEV)),
         ],
         compiler_params=pltpu.CompilerParams(
-            collective_id=0, has_side_effects=True, vmem_limit_bytes=62 * 1024 * 1024
+            collective_id=0, has_side_effects=True, vmem_limit_bytes=VMEM - 12058624
         ),
         name="route",
-    )(tokens, router.T, device_pick, expert_pick)
+    )(tokens, router.T, expert_pick)
     return pl.pallas_call(
         put,
         out_shape=outs[:2] + (jax.ShapeDtypeStruct((3,), f32),),

time: 51.2 us -> 46.5 us (0.908)
  Pallas kernels: 47.7 us -> 44.8 us
  local copies, waits for them, and re-layouts: 2.72 us -> 0.88 us
    pallas_call x1, Pallas kernels: 46.2 us -> 43.3 us  [local(): pl.pallas_call(kernel, out_shape=outs, in_specs=[pl.BlockSpec(memory_spac...]
    unnamed x6 -> x2, local copies, waits for them, and re-layouts: 2.72 us -> 0.88 us
where the time goes in v2:
time: 46.5 us; the launch traced here: 46.4 us
  Pallas kernels  44.8 us (96%)
  local copies, waits for them, and re-layouts  0.88 us (2%)
  between operations  0.65 us (1%)
    pallas_call x1, Pallas kernels, local(): pl.pallas_call(kernel, out_shape=outs, in_specs=[pl.BlockSpec(memory_spac...  43.3 us
    pallas_call x1, Pallas kernels, local(): pl.pallas_call(put, out_shape=outs[:2] + (jax.ShapeDtypeStruct((3,), f32)...  1.54 us

profile of v2, /device:TPU:1, one launch (start us, length us, event | category | flops | bytes accessed | tf_op | source)
XLA Modules:
  0.0 46.4 jit_solution(10449514783004092611)
XLA Ops:
  0.6 0.0 copy-start
  0.6 0.9 %copy-done = bf16[5120,5]{0,1:T(8,128)(2,1)S(1)} copy-done((bf16[5120,5]{0,1:T(8,128)(2,1)S(1)}, bf16[5120,5]{0,1:T(8,128)(2,1)}, u32[]{:S(2)}) %copy-start) | copy-done | bytes 51224
  1.5 43.3 %route.1 = (f32[6,32768]{1,0:T(8,128)S(1)}, f32[1,32768]{1,0:T(1,128)S(1)}, f32[1,128]{1,0:T(1,128)S(1)}) custom-call(bf16[5120,1024]{1,0:T(8,128)(2,1)} %tokens.1, bf16[5,5120]{1,0:T(8,128)(2,1)S(1)} %bitcast.1, s32[6,32768]{1,0:T(8,128)} %expert_pick.1), custom_call_target="tpu_custom_call" | custom-call | tf_op jit(solution)/shard_map/route/pallas_call | solution.py:438
  44.8 1.5 %put.1 = (f32[6,32768]{1,0:T(8,128)}, f32[1,32768]{1,0:T(1,128)}, f32[3]{0:T(128)}) custom-call(f32[6,32768]{1,0:T(8,128)S(1)} %get-tuple-element.6.gate_buf, f32[1,32768]{1,0:T(1,128)S(1)} %get-tuple-element.7.top_buf, f32[1,128]{1,0:T(1,128)S(1)} %get-tuple-element.8.sums), custom_call_target="tpu_custom_call" | custom-call | tf_op jit(solution)/shard_map/put/pallas_call | solution.py:483
Async XLA Ops:
  0.6 0.9 %copy-start = (bf16[5120,5]{0,1:T(8,128)(2,1)S(1)}, bf16[5120,5]{0,1:T(8,128)(2,1)}, u32[]{:S(2)}) copy-start(bf16[5120,5]{0,1:T(8,128)(2,1)} %param.5) | copy-start | bytes 153604

commit v3 on v2

--- a/solution.py
+++ b/solution.py
@@ -320,10 +320,11 @@
     result = jnp.zeros((1, 128), jnp.float32)
     for i in range(3):
         result = jnp.where(lane == i, whole(acc[i]) * scale[i], result)
-    bal_plane[me] = result
+    bal_plane[dp * NY + y] = result
 
     def plane_copy(i):
-        return send(bal_plane.at[me], bal_plane.at[me], bs.at[0, i], br.at[0, i], (dp, rem(me + i, NDEV)))
+        at = bal_plane.at[dp * NY + y]
+        return send(at, at, bs.at[0, i], br.at[0, i], (rem(dp + rem(i, NDP), NDP), z * NY + rem(y + i // NDP, NY)))
 
     def start_plane(i, carry):
         plane_copy(i).start()
@@ -354,18 +355,18 @@
             gate_z(j, c, False).wait_recv()
             for q in Y_ORDER:
                 gate_y(q, j, c).start()
+    def take_plane(i, carry):
+        plane_copy(i).wait_recv()
+        return carry
+
+    lax.fori_loop(1, NDEV, take_plane, 0)
+    bal_dp[z] = jnp.sum(bal_plane[...], axis=0)
+    bal_copies = [send(bal_dp.at[z], bal_dp.at[z], bs.at[1, j], br.at[1, j], z_peer(j)) for j in range(1, NZ)]
+    start(bal_copies)
     for c in range(CHUNKS):
         for j in (0,) + Z_ORDER:
             show(zz(j) * NY + y, c)
 
-    def take_plane(i, carry):
-        plane_copy(i).wait_recv()
-        return carry
-
-    lax.fori_loop(1, NDEV, take_plane, 0)
-    bal_dp[dp] = jnp.sum(bal_plane[...], axis=0)
-    bal_copies = [send(bal_dp.at[dp], bal_dp.at[dp], bs.at[1, i], br.at[1, i], dp_peer(i)) for i in range(1, NDP)]
-    start(bal_copies)
     for j in (0,) + Z_ORDER:
         for copy in z_copies(j) if j else ():
             copy.wait_send()
@@ -374,12 +375,23 @@
                 copy.wait_send()
     for copy in cnt_copies + cnt_z + cnt_y:
         copy.wait_send()
-    for c in range(CHUNKS):
+    def take_gates(c):
         for j in (0,) + Z_ORDER:
             for q in Y_ORDER:
                 gate_y(q, j, c, False).wait_recv()
                 show(zz(j) * NY + yy(q), c)
 
+    def gates_sent(c):
+        for j in (0,) + Z_ORDER:
+            if j:
+                gate_z(j, c).wait_send()
+            for q in Y_ORDER:
+                gate_y(q, j, c).wait_send()
+
+    for c in range(CHUNKS - 1):
+        take_gates(c)
+        gates_sent(c)
+
     def show_top(i, carry):
         src = rem(me + NDEV - i, NDEV)
 
@@ -393,24 +405,18 @@
         return carry
 
     lax.fori_loop(0, NDEV, show_top, 0)
-    arrive(bal_copies)
-    balance[...] = jnp.sum(bal_dp[...], axis=0)
-
-    for j in (0,) + Z_ORDER:
-        for c in range(CHUNKS):
-            if j:
-                gate_z(j, c).wait_send()
-            for q in Y_ORDER:
-                gate_y(q, j, c).wait_send()
-    for copy in bal_copies:
-        copy.wait_send()
-
     def sent_top(i, carry):
         top_copy(i).wait_send()
         plane_copy(i).wait_send()
         return carry
 
     lax.fori_loop(1, NDEV, sent_top, 0)
+    take_gates(CHUNKS - 1)
+    gates_sent(CHUNKS - 1)
+    arrive(bal_copies)
+    balance[...] = jnp.sum(bal_dp[...], axis=0)
+    for copy in bal_copies:
+        copy.wait_send()
 
 
 def put(gate_buf, top_buf, sums, gates, device_max, balance, sem):

time: 46.5 us -> 44.9 us (0.966)
  Pallas kernels: 44.8 us -> 43.3 us
    pallas_call x1, Pallas kernels: 43.3 us -> 41.7 us  [local(): pl.pallas_call(kernel, out_shape=outs, in_specs=[pl.BlockSpec(memory_spac...]
where the time goes in v3:
time: 44.9 us; the launch traced here: 44.8 us
  Pallas kernels  43.3 us (96%)
  local copies, waits for them, and re-layouts  0.88 us (2%)
  between operations  0.65 us (1%)
    pallas_call x1, Pallas kernels, local(): pl.pallas_call(kernel, out_shape=outs, in_specs=[pl.BlockSpec(memory_spac...  41.7 us
    pallas_call x1, Pallas kernels, local(): pl.pallas_call(put, out_shape=outs[:2] + (jax.ShapeDtypeStruct((3,), f32)...  1.54 us

profile of v3, /device:TPU:1, one launch (start us, length us, event | category | flops | bytes accessed | tf_op | source)
XLA Modules:
  0.0 44.8 jit_solution(1726693865417607324)
XLA Ops:
  0.6 0.0 copy-start
  0.6 0.9 %copy-done = bf16[5120,5]{0,1:T(8,128)(2,1)S(1)} copy-done((bf16[5120,5]{0,1:T(8,128)(2,1)S(1)}, bf16[5120,5]{0,1:T(8,128)(2,1)}, u32[]{:S(2)}) %copy-start) | copy-done | bytes 51224
  1.5 41.7 %route.1 = (f32[6,32768]{1,0:T(8,128)S(1)}, f32[1,32768]{1,0:T(1,128)S(1)}, f32[1,128]{1,0:T(1,128)S(1)}) custom-call(bf16[5120,1024]{1,0:T(8,128)(2,1)} %tokens.1, bf16[5,5120]{1,0:T(8,128)(2,1)S(1)} %bitcast.1, s32[6,32768]{1,0:T(8,128)} %expert_pick.1), custom_call_target="tpu_custom_call" | custom-call | tf_op jit(solution)/shard_map/route/pallas_call | solution.py:444
  43.3 1.5 %put.1 = (f32[6,32768]{1,0:T(8,128)}, f32[1,32768]{1,0:T(1,128)}, f32[3]{0:T(128)}) custom-call(f32[6,32768]{1,0:T(8,128)S(1)} %get-tuple-element.6.gate_buf, f32[1,32768]{1,0:T(1,128)S(1)} %get-tuple-element.7.top_buf, f32[1,128]{1,0:T(1,128)S(1)} %get-tuple-element.8.sums), custom_call_target="tpu_custom_call" | custom-call | tf_op jit(solution)/shard_map/put/pallas_call | solution.py:489
Async XLA Ops:
  0.6 0.9 %copy-start = (bf16[5120,5]{0,1:T(8,128)(2,1)S(1)}, bf16[5120,5]{0,1:T(8,128)(2,1)}, u32[]{:S(2)}) copy-start(bf16[5120,5]{0,1:T(8,128)(2,1)} %param.5) | copy-start | bytes 153604

commit v4 on v3

--- a/solution.py
+++ b/solution.py
@@ -72,6 +72,11 @@
             src_ref=src, dst_ref=dst, send_sem=s, recv_sem=r, device_id=device, device_id_type=MESH
         )
 
+    barrier = pltpu.get_barrier_semaphore()
+    friends = [z_peer(j) for j in (4, 3, 5, 2, 6, 1, 7)] + [y_peer(q) for q in Y_ORDER] + [dp_peer(i) for i in range(1, NDP)]
+    for device in friends:
+        pl.semaphore_signal(barrier, inc=1, device_id=device, device_id_type=MESH)
+
     pick_copy = pltpu.make_async_copy(expert_pick, picks, in_sem.at[0])
     pick_copy.start()
 
@@ -80,11 +85,6 @@
 
     for c in range(CHUNKS):
         token_copy(c).start()
-
-    barrier = pltpu.get_barrier_semaphore()
-    friends = [z_peer(j) for j in Z_ORDER] + [y_peer(q) for q in Y_ORDER] + [dp_peer(i) for i in range(1, NDP)]
-    for device in friends:
-        pl.semaphore_signal(barrier, inc=1, device_id=device, device_id_type=MESH)
 
     def tail_slot(zi, yi):
         return zi * NY + rem(yi, 2) * 2 + yi // 2

time: 44.9 us -> 44.9 us (level)
  no operation moved by 1% of the time
where the time goes in v4:
time: 44.9 us; the launch traced here: 44.8 us
  Pallas kernels  43.3 us (96%)
  local copies, waits for them, and re-layouts  0.88 us (2%)
  between operations  0.65 us (1%)
    pallas_call x1, Pallas kernels, local(): pl.pallas_call(kernel, out_shape=outs, in_specs=[pl.BlockSpec(memory_spac...  41.7 us
    pallas_call x1, Pallas kernels, local(): pl.pallas_call(put, out_shape=outs[:2] + (jax.ShapeDtypeStruct((3,), f32)...  1.54 us

profile of v4, /device:TPU:1, one launch (start us, length us, event | category | flops | bytes accessed | tf_op | source)
XLA Modules:
  0.0 44.8 jit_solution(10982468799921470485)
XLA Ops:
  0.6 0.0 copy-start
  0.6 0.9 %copy-done = bf16[5120,5]{0,1:T(8,128)(2,1)S(1)} copy-done((bf16[5120,5]{0,1:T(8,128)(2,1)S(1)}, bf16[5120,5]{0,1:T(8,128)(2,1)}, u32[]{:S(2)}) %copy-start) | copy-done | bytes 51224
  1.5 41.7 %route.1 = (f32[6,32768]{1,0:T(8,128)S(1)}, f32[1,32768]{1,0:T(1,128)S(1)}, f32[1,128]{1,0:T(1,128)S(1)}) custom-call(bf16[5120,1024]{1,0:T(8,128)(2,1)} %tokens.1, bf16[5,5120]{1,0:T(8,128)(2,1)S(1)} %bitcast.1, s32[6,32768]{1,0:T(8,128)} %expert_pick.1), custom_call_target="tpu_custom_call" | custom-call | tf_op jit(solution)/shard_map/route/pallas_call | solution.py:444
  43.3 1.5 %put.1 = (f32[6,32768]{1,0:T(8,128)}, f32[1,32768]{1,0:T(1,128)}, f32[3]{0:T(128)}) custom-call(f32[6,32768]{1,0:T(8,128)S(1)} %get-tuple-element.6.gate_buf, f32[1,32768]{1,0:T(1,128)S(1)} %get-tuple-element.7.top_buf, f32[1,128]{1,0:T(1,128)S(1)} %get-tuple-element.8.sums), custom_call_target="tpu_custom_call" | custom-call | tf_op jit(solution)/shard_map/put/pallas_call | solution.py:489
Async XLA Ops:
  0.6 0.9 %copy-start = (bf16[5120,5]{0,1:T(8,128)(2,1)S(1)}, bf16[5120,5]{0,1:T(8,128)(2,1)}, u32[]{:S(2)}) copy-start(bf16[5120,5]{0,1:T(8,128)(2,1)} %param.5) | copy-start | bytes 153604
